TPU v7x, 32 devices: a whole 2x2x4 slice. The times are simulated.
32 devices in a mesh: gx: 4 (over z), gy: 4 (over x, core), gz: 2 (over y).
Axes of the slice: x: 2, y: 2, z: 4, core: 2. Of those that a mesh axis runs over, the one named last changes fastest.
Arguments:
- right_side: bfloat16 [16, 256, 512], P('gz', 'gx', 'gy'), may hold values from -6 to 6
- phase_mask: int32 [16, 256, 512], P('gz', 'gx', 'gy'), may hold values from 0 to 1, as said below
Outputs:
- pressure: float32 [16, 256, 512], P('gz', 'gx', 'gy')
- scaled_residual: float32 [16, 256, 512], P('gz', 'gx', 'gy')
Inputs may be any that keep to these rules, and one draw needn't show every extreme that they name: `phase_mask`: 0 for a gas cell, 1 for a liquid cell.
All inputs are finite; a program needn't handle non-finite values.
Results may differ from a plain program's by a relative error of at most 0.0004.
Values may be sent and summed in bfloat16 or wider, within the bound.
A program may use at most 64 MiB of HBM per device.

v0:
```python
import jax
import jax.numpy as jnp
from jax import lax
from jax.sharding import PartitionSpec as P

ITERS = 3


density_ratio = 1000.0
mass_shift = 0.05


def padded_2(cells, sides, width):
    for axis, dim in sides:
        count = lax.axis_size(axis)
        head = lax.slice_in_dim(cells, 0, width, axis=dim)
        tail = lax.slice_in_dim(cells, cells.shape[dim] - width, cells.shape[dim], axis=dim)
        cells = jnp.concatenate(
            [
                lax.ppermute(tail, axis, [(i, (i + 1) % count) for i in range(count)]),
                cells,
                lax.ppermute(head, axis, [((i + 1) % count, i) for i in range(count)]),
            ],
            axis=dim,
        )
    return cells


def neighbour(padded, axis, start):
    window = [slice(1, -1), slice(1, -1), slice(1, -1)]
    length = padded.shape[axis] - 2
    window[axis] = slice(start, start + length)
    return padded[tuple(window)]


def centre(padded):
    return padded[1:-1, 1:-1, 1:-1]


def apply_padded(field, padded, weights):
    total = mass_shift * field
    for weight, axis, start in weights:
        total = total + weight * (field - neighbour(padded, axis, start))
    return total


def operate(field, weights):
    padded = padded_2(field, (("gx", 1), ("gy", 2), ("gz", 0)), 1)
    return apply_padded(field, padded, weights)


def products(first, second, third, fourth):
    return lax.psum((jnp.sum(first * second), jnp.sum(third * fourth)), ("gx", "gy", "gz"))


def build_weights(density_padded):
    density = centre(density_padded)
    weights = []
    diagonal = jnp.full(density.shape, mass_shift, jnp.float32)
    for axis in range(3):
        for start in (0, 2):
            weight = 2.0 / (density + neighbour(density_padded, axis, start))
            weights.append((weight, axis, start))
            diagonal = diagonal + weight
    return (weights, diagonal)


def on_device(right_side, phase_mask):
    mask_padded = padded_2(phase_mask, (("gx", 1), ("gy", 2), ("gz", 0)), 1)
    density_padded = 1.0 + (density_ratio - 1.0) * mask_padded.astype(jnp.float32)
    weights, diagonal = build_weights(density_padded)
    source = diagonal * right_side.astype(jnp.float32)
    smoothed = source / diagonal
    first_padded = padded_2(
        smoothed.astype(jnp.bfloat16), (("gx", 1), ("gy", 2), ("gz", 0)), 1
    ).astype(smoothed.dtype)
    applied = apply_padded(smoothed, first_padded, weights)
    pressure = jnp.zeros_like(source)
    residual = source
    direction = smoothed
    direction_image = applied
    scaled_update = smoothed
    twice_update = applied
    energy_old = jnp.float32(1.0)
    step_old = jnp.float32(1.0)
    for iteration in range(ITERS):
        energy, curvature = products(residual, smoothed, applied, smoothed)
        final_turn = iteration + 1 == ITERS
        if not final_turn:
            scaled_applied = applied / diagonal
            applied_twice = operate(scaled_applied, weights)
        if iteration == 0:
            step_size = energy / curvature
            direction = smoothed
            direction_image = applied
            scaled_update = scaled_applied
            twice_update = applied_twice
        else:
            factor = energy / energy_old
            step_size = energy / (curvature - factor * energy / step_old)
            direction = smoothed + factor * direction
            direction_image = applied + factor * direction_image
            if not final_turn:
                scaled_update = scaled_applied + factor * scaled_update
                twice_update = applied_twice + factor * twice_update
        pressure = pressure + step_size * direction
        residual = residual - step_size * direction_image
        if not final_turn:
            smoothed = smoothed - step_size * scaled_update
            applied = applied - step_size * twice_update
        energy_old = energy
        step_old = step_size
    return (pressure, residual / diagonal)


def solution(mesh):
    return jax.shard_map(
        on_device,
        mesh=mesh,
        in_specs=(P("gz", "gx", "gy"), P("gz", "gx", "gy")),
        out_specs=(P("gz", "gx", "gy"), P("gz", "gx", "gy")),
        check_vma=False,
    )
```

profile of v0, /device:TPU:0, one launch (start us, length us, event | category | flops | bytes accessed | tf_op | source)
XLA Modules:
  0.0 218.4 jit_solution(12359695470842941293)
XLA Ops:
  1.4 3.1 %collective-permute-start = (s32[8,1,128]{2,1,0:T(1,128)S(1)}, s32[8,1,128]{2,1,0:T(1,128)S(1)}, u32[]{:S(2)}, u32[]{:S(2)}) collective-permute-start(s32[8,1,128]{2,1,0:T(1,128)S(1)} %get-tuple-element.48), channel_id=1, source_target_pairs={{0,8},{8,16},{16,24},{24,0},{1,9},{9,17},{17,25},{25,1},{2,10},{10... | collective-permute-start | bytes 12296 | tf_op jit(solution)/shard_map/ppermute | solution.py:20
  4.5 2.1 collective-permute-start.1
  6.6 1.6 collective-permute-done
  9.3 1.7 collective-permute-start.3
  11.1 5.6 %collective-permute-done.2 = s32[8,66,1]{2,1,0:T(8,128)S(1)} collective-permute-done((s32[8,66,1]{2,1,0:T(8,128)S(1)}, s32[8,66,1]{2,1,0:T(8,128)S(1)}, u32[]{:S(2)}, u32[]{:S(2)}) %collective-permute-start.2) | collective-permute-done | bytes 2144 | tf_op jit(solution)/shard_map/ppermute | solution.py:20
  18.0 1.6 collective-permute-start.4
  20.0 2.9 %collective-permute-done.4 = s32[1,66,130]{2,1,0:T(8,128)S(1)} collective-permute-done((s32[1,66,130]{2,1,0:T(8,128)S(1)}, s32[1,66,130]{2,1,0:T(8,128)S(1)}, u32[]{:S(2)}, u32[]{:S(2)}) %collective-permute-start.4) | collective-permute-done | bytes 34352 | tf_op jit(solution)/shard_map/ppermute | solution.py:20
  23.0 1.4 collective-permute-done.5
  25.3 1.6 collective-permute-start.6
  26.9 2.4 %collective-permute-start.7 = (bf16[8,1,128]{2,1,0:T(2,128)(2,1)S(1)}, bf16[8,1,128]{2,1,0:T(2,128)(2,1)S(1)}, u32[]{:S(2)}, u32[]{:S(2)}) collective-permute-start(bf16[8,1,128]{2,1,0:T(2,128)(2,1)S(1)} %get-tuple-element.53), channel_id=1, source_target_pairs={{8,0},{16,8},{24,16},{0,24},{9,1},{17,9},{25,17},{1,25},{10,2},{18... | collective-permute-start | bytes 6152 | tf_op jit(solution)/shard_map/ppermute | solution.py:22
  29.2 1.5 collective-permute-done.6
  31.0 1.7 collective-permute-start.9
  32.7 2.8 %collective-permute-done.8 = bf16[8,66,1]{2,1,0:T(8,128)(2,1)S(1)} collective-permute-done((bf16[8,66,1]{2,1,0:T(8,128)(2,1)S(1)}, bf16[8,66,1]{2,1,0:T(8,128)(2,1)S(1)}, u32[]{:S(2)}, u32[]{:S(2)}) %collective-permute-start.8) | collective-permute-done | bytes 1088 | tf_op jit(solution)/shard_map/ppermute | solution.py:20
  36.4 1.6 collective-permute-start.10
  38.5 2.3 %collective-permute-done.10 = bf16[1,66,130]{2,1,0:T(8,128)(2,1)S(1)} collective-permute-done((bf16[1,66,130]{2,1,0:T(8,128)(2,1)S(1)}, bf16[1,66,130]{2,1,0:T(8,128)(2,1)S(1)}, u32[]{:S(2)}, u32[]{:S(2)}) %collective-permute-start.10) | collective-permute-done | bytes 17192 | tf_op jit(solution)/shard_map/ppermute | solution.py:20
  44.7 2.8 %collective-permute-start.13 = (f32[8,1,128]{2,1,0:T(1,128)S(1)}, f32[8,1,128]{2,1,0:T(1,128)S(1)}, u32[]{:S(2)}, u32[]{:S(2)}) collective-permute-start(f32[8,1,128]{2,1,0:T(1,128)S(1)} %get-tuple-element.47), channel_id=1, source_target_pairs={{8,0},{16,8},{24,16},{0,24},{9,1},{17,9},{25,17},{1,25},{10,2},{18... | collective-permute-start | bytes 12296 | tf_op jit(solution)/shard_map/ppermute | solution.py:22
  47.5 1.5 collective-permute-done.12
  49.3 1.7 collective-permute-start.15
  51.0 5.7 %collective-permute-done.14 = f32[8,66,1]{2,1,0:T(8,128)S(1)} collective-permute-done((f32[8,66,1]{2,1,0:T(8,128)S(1)}, f32[8,66,1]{2,1,0:T(8,128)S(1)}, u32[]{:S(2)}, u32[]{:S(2)}) %collective-permute-start.14) | collective-permute-done | bytes 2144 | tf_op jit(solution)/shard_map/ppermute | solution.py:20
  60.4 40.0 %all-reduce.2 = (f32[]{:T(128)}, f32[]{:T(128)}) all-reduce(f32[]{:T(128)} %get-tuple-element.5, f32[]{:T(128)} %get-tuple-element.4), channel_id=1, replica_groups=mesh['gx'=4,'gy'=4,'gz'=2] {'gx','gy','gz'}, use_global_device_ids=true, to_apply=%region_1.0 | all-reduce | flops 2 | bytes 16 | tf_op jit(solution)/shard_map/psum | solution.py:53
  101.7 1.5 fusion.60
  103.2 1.9 collective-permute-start.18
  105.1 2.0 collective-permute-start.19
  107.1 1.6 collective-permute-done.18
  109.0 1.7 collective-permute-start.21
  110.7 5.0 %collective-permute-done.20 = f32[8,66,1]{2,1,0:T(8,128)S(1)} collective-permute-done((f32[8,66,1]{2,1,0:T(8,128)S(1)}, f32[8,66,1]{2,1,0:T(8,128)S(1)}, u32[]{:S(2)}, u32[]{:S(2)}) %collective-permute-start.20) | collective-permute-done | bytes 2144 | tf_op jit(solution)/shard_map/ppermute | solution.py:20
  115.7 2.4 %collective-permute-done.21 = f32[8,66,1]{2,1,0:T(8,128)S(1)} collective-permute-done((f32[8,66,1]{2,1,0:T(8,128)S(1)}, f32[8,66,1]{2,1,0:T(8,128)S(1)}, u32[]{:S(2)}, u32[]{:S(2)}) %collective-permute-start.21) | collective-permute-done | bytes 2144 | tf_op jit(solution)/shard_map/ppermute | solution.py:22
  118.8 1.5 collective-permute-start.22
  121.6 40.3 %all-reduce.1 = (f32[]{:T(128)}, f32[]{:T(128)}) all-reduce(f32[]{:T(128)} %get-tuple-element.3, f32[]{:T(128)} %get-tuple-element.2), channel_id=1, replica_groups=mesh['gx'=4,'gy'=4,'gz'=2] {'gx','gy','gz'}, use_global_device_ids=true, to_apply=%region_5.0 | all-reduce | flops 2 | bytes 16 | tf_op jit(solution)/shard_map/psum | solution.py:53
  167.2 3.3 %multiply_reduce_fusion = (f32[]{:T(128)}, f32[]{:T(128)}, f32[8,64,128]{2,1,0:T(8,128)S(1)}, f32[8,64,128]{2,1,0:T(8,128)}) fusion(f32[8,64,128]{2,1,0:T(8,128)S(1)} %get-tuple-element.18, f32[8,64,128]{2,1,0:T(8,128)S(1)} %get-tuple-element.19, f32[]{:T(128)S(6)} %div.60, f32[8,64,128]{2,1,0:T(8,128)S(1)} %get-tuple-element.17, f32[]{:T(128)S(6)} %div.58, ...), kind=kLoop, calls=%fused_computation.114 | loop fusion | flops 3997694 | bytes 3882164 | tf_op jit(solution)/shard_map/reduce_sum | solution.py:53
  170.4 42.1 %all-reduce = (f32[]{:T(128)}, f32[]{:T(128)}) all-reduce(f32[]{:T(128)} %get-tuple-element.7, f32[]{:T(128)} %get-tuple-element.6), channel_id=1, replica_groups=mesh['gx'=4,'gy'=4,'gz'=2] {'gx','gy','gz'}, use_global_device_ids=true, to_apply=%region_9.0 | all-reduce | flops 2 | bytes 16 | tf_op jit(solution)/shard_map/psum | solution.py:53
  216.4 2.0 subtract_divide_fusion
  (56 shorter events, 16.9 us)
Async XLA Ops:
  1.4 6.7 %collective-permute-start = (s32[8,1,128]{2,1,0:T(1,128)S(1)}, s32[8,1,128]{2,1,0:T(1,128)S(1)}, u32[]{:S(2)}, u32[]{:S(2)}) collective-permute-start(s32[8,1,128]{2,1,0:T(1,128)S(1)} %get-tuple-element.48), channel_id=1, source_target_pairs={{0,8},{8,16},{16,24},{24,0},{1,9},{9,17},{17,25},{25,1},{2,10},{10... | collective-permute-start | bytes 12296 | tf_op jit(solution)/shard_map/ppermute | solution.py:20
  4.5 3.7 %collective-permute-start.1 = (s32[8,1,128]{2,1,0:T(1,128)S(1)}, s32[8,1,128]{2,1,0:T(1,128)S(1)}, u32[]{:S(2)}, u32[]{:S(2)}) collective-permute-start(s32[8,1,128]{2,1,0:T(1,128)S(1)} %get-tuple-element.49), channel_id=1, source_target_pairs={{8,0},{16,8},{24,16},{0,24},{9,1},{17,9},{25,17},{1,25},{10,2},{18... | collective-permute-start | bytes 12296 | tf_op jit(solution)/shard_map/ppermute | solution.py:22
  9.1 8.7 %copy-start.1 = (s32[8,64,128]{2,1,0:T(8,128)S(1)}, s32[8,64,128]{2,1,0:T(8,128)}, u32[]{:S(2)}) copy-start(s32[8,64,128]{2,1,0:T(8,128)} %param.3) | copy-start | bytes 786436
  9.3 7.4 %collective-permute-start.2 = (s32[8,66,1]{2,1,0:T(8,128)S(1)}, s32[8,66,1]{2,1,0:T(8,128)S(1)}, u32[]{:S(2)}, u32[]{:S(2)}) collective-permute-start(s32[8,66,1]{2,1,0:T(8,128)S(1)} %get-tuple-element.40), channel_id=1, source_target_pairs={{0,2},{2,4},{4,6},{6,0},{1,3},{3,5},{5,7},{7,1},{8,10},{10,12},{12... | collective-permute-start | bytes 6344 | tf_op jit(solution)/shard_map/ppermute | solution.py:20
  9.3 8.5 %collective-permute-start.3 = (s32[8,66,1]{2,1,0:T(8,128)S(1)}, s32[8,66,1]{2,1,0:T(8,128)S(1)}, u32[]{:S(2)}, u32[]{:S(2)}) collective-permute-start(s32[8,66,1]{2,1,0:T(8,128)S(1)} %get-tuple-element.41), channel_id=1, source_target_pairs={{2,0},{4,2},{6,4},{0,6},{3,1},{5,3},{7,5},{1,7},{10,8},{12,10},{14... | collective-permute-start | bytes 6344 | tf_op jit(solution)/shard_map/ppermute | solution.py:22
  18.0 5.0 %collective-permute-start.4 = (s32[1,66,130]{2,1,0:T(8,128)S(1)}, s32[1,66,130]{2,1,0:T(8,128)S(1)}, u32[]{:S(2)}, u32[]{:S(2)}) collective-permute-start(s32[1,66,130]{2,1,0:T(8,128)S(1)} %get-tuple-element.32), channel_id=1, source_target_pairs={{0,1},{1,0},{2,3},{3,2},{4,5},{5,4},{6,7},{7,6},{8,9},{9,8},{10,11... | collective-permute-start | bytes 102968 | tf_op jit(solution)/shard_map/ppermute | solution.py:20
  19.5 5.2 %copy-start = (bf16[8,64,128]{2,1,0:T(8,128)(2,1)S(1)}, bf16[8,64,128]{2,1,0:T(8,128)(2,1)}, u32[]{:S(2)}) copy-start(bf16[8,64,128]{2,1,0:T(8,128)(2,1)} %param.2) | copy-start | bytes 393220
  19.5 4.9 %collective-permute-start.5 = (s32[1,66,130]{2,1,0:T(8,128)S(1)}, s32[1,66,130]{2,1,0:T(8,128)S(1)}, u32[]{:S(2)}, u32[]{:S(2)}) collective-permute-start(s32[1,66,130]{2,1,0:T(8,128)S(1)} %get-tuple-element.33), channel_id=1, source_target_pairs={{1,0},{0,1},{3,2},{2,3},{5,4},{4,5},{7,6},{6,7},{9,8},{8,9},{11,10... | collective-permute-start | bytes 102968 | tf_op jit(solution)/shard_map/ppermute | solution.py:22
  25.3 5.5 %collective-permute-start.6 = (bf16[8,1,128]{2,1,0:T(2,128)(2,1)S(1)}, bf16[8,1,128]{2,1,0:T(2,128)(2,1)S(1)}, u32[]{:S(2)}, u32[]{:S(2)}) collective-permute-start(bf16[8,1,128]{2,1,0:T(2,128)(2,1)S(1)} %get-tuple-element.52), channel_id=1, source_target_pairs={{0,8},{8,16},{16,24},{24,0},{1,9},{9,17},{17,25},{25,1},{2,10},{10... | collective-permute-start | bytes 6152 | tf_op jit(solution)/shard_map/ppermute | solution.py:20
  26.9 3.9 %collective-permute-start.7 = (bf16[8,1,128]{2,1,0:T(2,128)(2,1)S(1)}, bf16[8,1,128]{2,1,0:T(2,128)(2,1)S(1)}, u32[]{:S(2)}, u32[]{:S(2)}) collective-permute-start(bf16[8,1,128]{2,1,0:T(2,128)(2,1)S(1)} %get-tuple-element.53), channel_id=1, source_target_pairs={{8,0},{16,8},{24,16},{0,24},{9,1},{17,9},{25,17},{1,25},{10,2},{18... | collective-permute-start | bytes 6152 | tf_op jit(solution)/shard_map/ppermute | solution.py:22
  30.9 4.6 %collective-permute-start.8 = (bf16[8,66,1]{2,1,0:T(8,128)(2,1)S(1)}, bf16[8,66,1]{2,1,0:T(8,128)(2,1)S(1)}, u32[]{:S(2)}, u32[]{:S(2)}) collective-permute-start(bf16[8,66,1]{2,1,0:T(8,128)(2,1)S(1)} %get-tuple-element.50), channel_id=1, source_target_pairs={{0,2},{2,4},{4,6},{6,0},{1,3},{3,5},{5,7},{7,1},{8,10},{10,12},{12... | collective-permute-start | bytes 3176 | tf_op jit(solution)/shard_map/ppermute | solution.py:20
  31.0 5.3 %collective-permute-start.9 = (bf16[8,66,1]{2,1,0:T(8,128)(2,1)S(1)}, bf16[8,66,1]{2,1,0:T(8,128)(2,1)S(1)}, u32[]{:S(2)}, u32[]{:S(2)}) collective-permute-start(bf16[8,66,1]{2,1,0:T(8,128)(2,1)S(1)} %get-tuple-element.51), channel_id=1, source_target_pairs={{2,0},{4,2},{6,4},{0,6},{3,1},{5,3},{7,5},{1,7},{10,8},{12,10},{14... | collective-permute-start | bytes 3176 | tf_op jit(solution)/shard_map/ppermute | solution.py:22
  36.4 4.4 %collective-permute-start.10 = (bf16[1,66,130]{2,1,0:T(8,128)(2,1)S(1)}, bf16[1,66,130]{2,1,0:T(8,128)(2,1)S(1)}, u32[]{:S(2)}, u32[]{:S(2)}) collective-permute-start(bf16[1,66,130]{2,1,0:T(8,128)(2,1)S(1)} %get-tuple-element.34), channel_id=1, source_target_pairs={{0,1},{1,0},{2,3},{3,2},{4,5},{5,4},{6,7},{7,6},{8,9},{9,8},{10,11... | collective-permute-start | bytes 51488 | tf_op jit(solution)/shard_map/ppermute | solution.py:20
  38.0 4.1 %collective-permute-start.11 = (bf16[1,66,130]{2,1,0:T(8,128)(2,1)S(1)}, bf16[1,66,130]{2,1,0:T(8,128)(2,1)S(1)}, u32[]{:S(2)}, u32[]{:S(2)}) collective-permute-start(bf16[1,66,130]{2,1,0:T(8,128)(2,1)S(1)} %get-tuple-element.35), channel_id=1, source_target_pairs={{1,0},{0,1},{3,2},{2,3},{5,4},{4,5},{7,6},{6,7},{9,8},{8,9},{11,10... | collective-permute-start | bytes 51488 | tf_op jit(solution)/shard_map/ppermute | solution.py:22
  43.5 5.5 %collective-permute-start.12 = (f32[8,1,128]{2,1,0:T(1,128)S(1)}, f32[8,1,128]{2,1,0:T(1,128)S(1)}, u32[]{:S(2)}, u32[]{:S(2)}) collective-permute-start(f32[8,1,128]{2,1,0:T(1,128)S(1)} %get-tuple-element.46), channel_id=1, source_target_pairs={{0,8},{8,16},{16,24},{24,0},{1,9},{9,17},{17,25},{25,1},{2,10},{10... | collective-permute-start | bytes 12296 | tf_op jit(solution)/shard_map/ppermute | solution.py:20
  44.7 4.3 %collective-permute-start.13 = (f32[8,1,128]{2,1,0:T(1,128)S(1)}, f32[8,1,128]{2,1,0:T(1,128)S(1)}, u32[]{:S(2)}, u32[]{:S(2)}) collective-permute-start(f32[8,1,128]{2,1,0:T(1,128)S(1)} %get-tuple-element.47), channel_id=1, source_target_pairs={{8,0},{16,8},{24,16},{0,24},{9,1},{17,9},{25,17},{1,25},{10,2},{18... | collective-permute-start | bytes 12296 | tf_op jit(solution)/shard_map/ppermute | solution.py:22
  49.2 7.5 %collective-permute-start.14 = (f32[8,66,1]{2,1,0:T(8,128)S(1)}, f32[8,66,1]{2,1,0:T(8,128)S(1)}, u32[]{:S(2)}, u32[]{:S(2)}) collective-permute-start(f32[8,66,1]{2,1,0:T(8,128)S(1)} %get-tuple-element.38), channel_id=1, source_target_pairs={{0,2},{2,4},{4,6},{6,0},{1,3},{3,5},{5,7},{7,1},{8,10},{10,12},{12... | collective-permute-start | bytes 6344 | tf_op jit(solution)/shard_map/ppermute | solution.py:20
  49.3 8.3 %collective-permute-start.15 = (f32[8,66,1]{2,1,0:T(8,128)S(1)}, f32[8,66,1]{2,1,0:T(8,128)S(1)}, u32[]{:S(2)}, u32[]{:S(2)}) collective-permute-start(f32[8,66,1]{2,1,0:T(8,128)S(1)} %get-tuple-element.39), channel_id=1, source_target_pairs={{2,0},{4,2},{6,4},{0,6},{3,1},{5,3},{7,5},{1,7},{10,8},{12,10},{14... | collective-permute-start | bytes 6344 | tf_op jit(solution)/shard_map/ppermute | solution.py:22
  57.6 0.7 copy-start.4
  58.3 43.4 %collective-permute-start.16 = (f32[1,66,130]{2,1,0:T(8,128)S(1)}, f32[1,66,130]{2,1,0:T(8,128)S(1)}, u32[]{:S(2)}, u32[]{:S(2)}) collective-permute-start(f32[1,66,130]{2,1,0:T(8,128)S(1)} %get-tuple-element.30), channel_id=1, source_target_pairs={{0,1},{1,0},{2,3},{3,2},{4,5},{5,4},{6,7},{7,6},{8,9},{9,8},{10,11... | collective-permute-start | bytes 102968 | tf_op jit(solution)/shard_map/ppermute | solution.py:20
  59.2 42.6 %collective-permute-start.17 = (f32[1,66,130]{2,1,0:T(8,128)S(1)}, f32[1,66,130]{2,1,0:T(8,128)S(1)}, u32[]{:S(2)}, u32[]{:S(2)}) collective-permute-start(f32[1,66,130]{2,1,0:T(8,128)S(1)} %get-tuple-element.31), channel_id=1, source_target_pairs={{1,0},{0,1},{3,2},{2,3},{5,4},{4,5},{7,6},{6,7},{9,8},{8,9},{11,10... | collective-permute-start | bytes 102968 | tf_op jit(solution)/shard_map/ppermute | solution.py:22
  103.2 5.5 %collective-permute-start.18 = (f32[8,1,128]{2,1,0:T(1,128)S(1)}, f32[8,1,128]{2,1,0:T(1,128)S(1)}, u32[]{:S(2)}, u32[]{:S(2)}) collective-permute-start(f32[8,1,128]{2,1,0:T(1,128)S(1)} %get-tuple-element.44), channel_id=1, source_target_pairs={{0,8},{8,16},{16,24},{24,0},{1,9},{9,17},{17,25},{25,1},{2,10},{10... | collective-permute-start | bytes 12296 | tf_op jit(solution)/shard_map/ppermute | solution.py:20
  105.1 3.6 %collective-permute-start.19 = (f32[8,1,128]{2,1,0:T(1,128)S(1)}, f32[8,1,128]{2,1,0:T(1,128)S(1)}, u32[]{:S(2)}, u32[]{:S(2)}) collective-permute-start(f32[8,1,128]{2,1,0:T(1,128)S(1)} %get-tuple-element.45), channel_id=1, source_target_pairs={{8,0},{16,8},{24,16},{0,24},{9,1},{17,9},{25,17},{1,25},{10,2},{18... | collective-permute-start | bytes 12296 | tf_op jit(solution)/shard_map/ppermute | solution.py:22
  108.9 6.8 %collective-permute-start.20 = (f32[8,66,1]{2,1,0:T(8,128)S(1)}, f32[8,66,1]{2,1,0:T(8,128)S(1)}, u32[]{:S(2)}, u32[]{:S(2)}) collective-permute-start(f32[8,66,1]{2,1,0:T(8,128)S(1)} %get-tuple-element.36), channel_id=1, source_target_pairs={{0,2},{2,4},{4,6},{6,0},{1,3},{3,5},{5,7},{7,1},{8,10},{10,12},{12... | collective-permute-start | bytes 6344 | tf_op jit(solution)/shard_map/ppermute | solution.py:20
  109.0 9.1 %collective-permute-start.21 = (f32[8,66,1]{2,1,0:T(8,128)S(1)}, f32[8,66,1]{2,1,0:T(8,128)S(1)}, u32[]{:S(2)}, u32[]{:S(2)}) collective-permute-start(f32[8,66,1]{2,1,0:T(8,128)S(1)} %get-tuple-element.37), channel_id=1, source_target_pairs={{2,0},{4,2},{6,4},{0,6},{3,1},{5,3},{7,5},{1,7},{10,8},{12,10},{14... | collective-permute-start | bytes 6344 | tf_op jit(solution)/shard_map/ppermute | solution.py:22
  115.7 2.5 %copy-start.2 = (f32[8,66,1]{2,1,0:T(8,128)}, f32[8,66,1]{2,1,0:T(8,128)S(1)}, u32[]{:S(2)}) copy-start(f32[8,66,1]{2,1,0:T(8,128)S(1)} %collective-permute-done.20) | copy-start | bytes 6340
  118.1 0.7 copy-start.3
  118.8 47.7 %collective-permute-start.22 = (f32[1,66,130]{2,1,0:T(8,128)S(1)}, f32[1,66,130]{2,1,0:T(8,128)S(1)}, u32[]{:S(2)}, u32[]{:S(2)}) collective-permute-start(f32[1,66,130]{2,1,0:T(8,128)S(1)} %get-tuple-element.28), channel_id=1, source_target_pairs={{0,1},{1,0},{2,3},{3,2},{4,5},{5,4},{6,7},{7,6},{8,9},{9,8},{10,11... | collective-permute-start | bytes 102968 | tf_op jit(solution)/shard_map/ppermute | solution.py:20
  120.3 46.3 %collective-permute-start.23 = (f32[1,66,130]{2,1,0:T(8,128)S(1)}, f32[1,66,130]{2,1,0:T(8,128)}, u32[]{:S(2)}, u32[]{:S(2)}) collective-permute-start(f32[1,66,130]{2,1,0:T(8,128)S(1)} %get-tuple-element.29), channel_id=1, source_target_pairs={{1,0},{0,1},{3,2},{2,3},{5,4},{4,5},{7,6},{6,7},{9,8},{8,9},{11,10... | collective-permute-start | bytes 102968 | tf_op jit(solution)/shard_map/ppermute | solution.py:22
  166.5 0.6 copy-start.5
where the time goes:
time: 219 us; the launch traced here: 218 us
  blocking collectives  122 us (56%)
  waiting for transfers between devices  38.5 us (18%)
  starting transfers between devices  32.4 us (15%)
  other arithmetic  11.3 us (5%)
  between operations  10.7 us (5%)
  local copies, waits for them, and re-layouts  3.12 us (1%)
    psum x3, blocking collectives, products(): lax.psum((jnp.sum(first * second), jnp.sum(third * fourth)), ('gx', 'gy',...  122 us
    ppermute x12, waiting for transfers between devices, padded_2(): lax.ppermute(tail, axis, [(i, (i + 1) % count) for i in range(count)])  30.6 us
    ppermute x12, starting transfers between devices, padded_2(): lax.ppermute(head, axis, [((i + 1) % count, i) for i in range(count)])  19 us
    ppermute x12, starting transfers between devices, padded_2(): lax.ppermute(tail, axis, [(i, (i + 1) % count) for i in range(count)])  13.4 us
    ppermute x12, waiting for transfers between devices, padded_2(): lax.ppermute(head, axis, [((i + 1) % count, i) for i in range(count)])  7.98 us
    reduce_sum x3, other arithmetic, products(): jnp.sum(third * fourth)  5.16 us
  transfers between devices with their start and end apart: 24, of which 17 were waited for; matrix products, arithmetic and copies ran while one was open for 0% of the time, Pallas kernels for 0%

commit v1 on v0

v1 whole, which is shorter than its diff:
```python
import functools
import itertools

import jax
import jax.numpy as jnp
from jax import lax
from jax.experimental import pallas as pl
from jax.experimental.pallas import tpu as pltpu
from jax.sharding import PartitionSpec as P

ITERS = 3
AXES = ("gx", "gy", "gz")
MESH = pl.DeviceIdType.MESH
F32 = jnp.float32

density_gas = 1.0
density_liquid = 1000.0
mass_shift = 0.05


def shifted(sizes, offsets):
    return {
        axis: lax.rem(lax.axis_index(axis) + offset, sizes[axis])
        for axis, offset in offsets.items()
        if offset
    }


def group_offsets(sizes, group):
    spans = [range(sizes[axis]) for axis in group]
    return [dict(zip(group, point)) for point in itertools.product(*spans) if any(point)]


def exchange(sizes, phase, faces, landings, send_sems, recv_sems):
    copies = []
    for place, (axis, (low, high), (from_below, from_above)) in enumerate(
        zip(("gz", "gx", "gy"), faces, landings)
    ):
        for side, source, target, offset in (
            (0, high, from_below, 1),
            (1, low, from_above, sizes[axis] - 1),
        ):
            copy = pltpu.make_async_remote_copy(
                src_ref=source,
                dst_ref=target,
                send_sem=send_sems.at[phase, 2 * place + side],
                recv_sem=recv_sems.at[phase, 2 * place + side],
                device_id=shifted(sizes, {axis: offset}),
                device_id_type=MESH,
            )
            copy.start()
            copies.append(copy)
    return copies


def polynomial_sum(first, second, factor):
    length = max(len(first), len(second))
    out = []
    for i in range(length):
        if i >= len(second):
            out.append(first[i])
        elif i >= len(first):
            out.append(factor * second[i])
        else:
            out.append(first[i] + factor * second[i])
    return out


def gradient_coefficients(moments):
    one, zero = jnp.ones_like(moments[0]), jnp.zeros_like(moments[0])

    def inner(first, second, weights):
        total = None
        for i, a in enumerate(first):
            for j, b in enumerate(second):
                term = a * b * weights[i + j]
                total = term if total is None else total + term
        return total

    drops = [moments[i] - moments[i + 1] for i in range(len(moments) - 1)]
    residual, direction, pressure = [one], [one], []
    energy = moments[0]
    for iteration in range(ITERS):
        step = energy / inner(direction, direction, drops)
        pressure = polynomial_sum(pressure, direction, step)
        image = polynomial_sum(direction, [zero] + direction, -1.0)
        residual = polynomial_sum(residual, image, -step)
        if iteration + 1 < ITERS:
            fresh = inner(residual, residual, moments)
            direction = polynomial_sum(residual, direction, fresh / energy)
            energy = fresh
    return pressure, residual


def kernel(
    sizes, groups, right_ref, mask_ref, pressure_ref, scaled_ref,
    fields, phases, coefs, diag, sz0, sx0, rz0, rx0, sx, sy, rz, rx, ry,
    partial, gathered, send_sems, recv_sems, sum_send, sum_recv,
):
    depth, rows, lanes = right_ref.shape
    peers = []
    for offset in [dict([(a, o)]) for a in AXES for o in (1, sizes[a] - 1)] + [
        o for group in groups for o in group_offsets(sizes, group)
    ]:
        if offset not in peers:
            peers.append(offset)
    barrier = pltpu.get_barrier_semaphore()
    for offset in peers:
        pl.semaphore_signal(barrier, inc=1, device_id=shifted(sizes, offset), device_id_type=MESH)

    row = lax.broadcasted_iota(jnp.int32, (rows, lanes), 0)
    lane = lax.broadcasted_iota(jnp.int32, (rows, lanes), 1)
    even = lane % 2 == 0

    def pack(packed, plane, z, base):
        at = base + 2 * z
        turned = pltpu.roll(plane, (at + 1) % lanes, 1)
        return jnp.where((lane == at) | (lane == at + 1), turned, packed)

    def unpack(below, above):
        return jnp.where(even, pltpu.roll(above, lanes - 1, 1), pltpu.roll(below, 1, 1))

    def neighbours(plane, under, over, low_row, high_row, sides, z, base):
        at = base + 2 * z
        edge = pltpu.roll(sides, (lanes - at - 1) % lanes, 1)
        return (
            under,
            over,
            jnp.where(row == 0, low_row, pltpu.roll(plane, 1, 0)),
            jnp.where(row == rows - 1, high_row, pltpu.roll(plane, rows - 1, 0)),
            jnp.where(lane == 0, edge, pltpu.roll(plane, 1, 1)),
            jnp.where(lane == lanes - 1, edge, pltpu.roll(plane, lanes - 1, 1)),
        )

    packed = jnp.zeros((rows, lanes), F32)
    for z in range(depth):
        value = right_ref[z].astype(F32)
        phase = mask_ref[z].astype(F32)
        fields[0, z] = value
        phases[z] = phase
        packed = pack(packed, value, z, 0)
        packed = pack(packed, phase, z, 2 * depth)
        for part, plane in enumerate((value, phase)):
            sx0[0, part, z : z + 1, :] = plane[0:1]
            sx0[1, part, z : z + 1, :] = plane[rows - 1 : rows]
        for side, face in ((0, 0), (1, depth - 1)):
            if z == face:
                sz0[side, 0] = right_ref[z]
                sz0[side, 1] = phase.astype(jnp.bfloat16)
    sy[0] = packed
    pl.semaphore_wait(barrier, len(peers))

    copies = exchange(
        sizes,
        0,
        ((sz0.at[0], sz0.at[1]), (sx0.at[0], sx0.at[1]), (sy.at[0], sy.at[0])),
        ((rz0.at[0], rz0.at[1]), (rx0.at[0], rx0.at[1]), (ry.at[0, 0], ry.at[0, 1])),
        send_sems,
        recv_sems,
    )
    for copy in copies:
        copy.wait()

    def fold(product):
        return jnp.sum(product.reshape(rows // 8, 8, lanes), axis=0)

    sums = [jnp.zeros((8, lanes), F32) for _ in range(2 * ITERS)]
    mixed = 2.0 / (density_gas + density_liquid)
    for phase in range(ITERS):
        sides = unpack(ry[phase, 0], ry[phase, 1])
        packed = jnp.zeros((rows, lanes), F32)
        for z in range(depth):
            if phase == 0:
                below = rz0[0, 1].astype(F32) if z == 0 else phases[z - 1]
                above = rz0[1, 1].astype(F32) if z == depth - 1 else phases[z + 1]
                own = phases[z]
                around = neighbours(
                    own, below, above,
                    rx0[0, 1, z : z + 1, :], rx0[1, 1, z : z + 1, :], sides, z, 2 * depth,
                )
                weights = []
                diagonal = jnp.full((rows, lanes), mass_shift, F32)
                for other in around:
                    count = own + other
                    weight = jnp.where(
                        count < 0.5,
                        1.0 / density_gas,
                        jnp.where(count < 1.5, mixed, 1.0 / density_liquid),
                    )
                    weights.append(weight)
                    diagonal = diagonal + weight
                diag[z] = diagonal
                inverse = 1.0 / diagonal
                weights = [weight * inverse for weight in weights]
                for k, weight in enumerate(weights):
                    coefs[k, z] = weight
                below = rz0[0, 0].astype(F32) if z == 0 else fields[0, z - 1]
                above = rz0[1, 0].astype(F32) if z == depth - 1 else fields[0, z + 1]
                low, high = rx0[0, 0, z : z + 1, :], rx0[1, 0, z : z + 1, :]
            else:
                diagonal = diag[z]
                weights = [coefs[k, z] for k in range(6)]
                below = rz[phase - 1, 0] if z == 0 else fields[phase, z - 1]
                above = rz[phase - 1, 1] if z == depth - 1 else fields[phase, z + 1]
                low, high = rx[phase - 1, 0, z : z + 1, :], rx[phase - 1, 1, z : z + 1, :]
            own = fields[phase, z]
            around = neighbours(own, below, above, low, high, sides, z, 0)
            mean = weights[0] * around[0]
            for weight, other in zip(weights[1:], around[1:]):
                mean = mean + weight * other
            fields[phase + 1, z] = mean
            scaled = diagonal * own
            sums[2 * phase] = sums[2 * phase] + fold(scaled * own)
            sums[2 * phase + 1] = sums[2 * phase + 1] + fold(scaled * mean)
            if phase + 1 < ITERS:
                packed = pack(packed, mean, z, 0)
                sx[phase, 0, z : z + 1, :] = mean[0:1]
                sx[phase, 1, z : z + 1, :] = mean[rows - 1 : rows]
        if phase + 1 < ITERS:
            sy[phase + 1] = packed
            copies = exchange(
                sizes,
                phase + 1,
                (
                    (fields.at[phase + 1, 0], fields.at[phase + 1, depth - 1]),
                    (sx.at[phase, 0], sx.at[phase, 1]),
                    (sy.at[phase + 1], sy.at[phase + 1]),
                ),
                (
                    (rz.at[phase, 0], rz.at[phase, 1]),
                    (rx.at[phase, 0], rx.at[phase, 1]),
                    (ry.at[phase + 1, 0], ry.at[phase + 1, 1]),
                ),
                send_sems,
                recv_sems,
            )
            for copy in copies:
                copy.wait()

    line = lax.broadcasted_iota(jnp.int32, (8, lanes), 0)
    tile = jnp.zeros((8, lanes), F32)
    for k, total in enumerate(sums):
        tile = jnp.where(line == k, jnp.sum(total, axis=0, keepdims=True), tile)
    slot = 0
    for number, group in enumerate(groups):
        partial[number] = tile
        copies = []
        first = slot
        for offset in group_offsets(sizes, group):
            copy = pltpu.make_async_remote_copy(
                src_ref=partial.at[number],
                dst_ref=gathered.at[slot],
                send_sem=sum_send.at[slot],
                recv_sem=sum_recv.at[slot],
                device_id=shifted(sizes, offset),
                device_id_type=MESH,
            )
            copy.start()
            copies.append(copy)
            slot += 1
        for copy in copies:
            copy.wait()
        for k in range(first, slot):
            tile = tile + gathered[k]

    whole = jnp.sum(tile, axis=1, keepdims=True)
    moments = [whole[k : k + 1] for k in range(2 * ITERS)]
    pressure, residual = gradient_coefficients(moments)
    for z in range(depth):
        basis = [fields[k, z] for k in range(ITERS + 1)]
        for ref, factors in ((pressure_ref, pressure), (scaled_ref, residual)):
            total = factors[0] * basis[0]
            for factor, part in zip(factors[1:], basis[1:]):
                total = total + factor * part
            ref[z] = total


def choose_groups(sizes, most=32):
    groups = []
    for axis in ("gz", "gy", "gx"):
        if groups and sizes[axis] * functools.reduce(lambda n, a: n * sizes[a], groups[-1], 1) <= most:
            groups[-1] = groups[-1] + (axis,)
        else:
            groups.append((axis,))
    return tuple(groups)


def solution(mesh):
    sizes = {axis: mesh.shape[axis] for axis in AXES}
    groups = choose_groups(sizes, 8)
    slots = sum(len(group_offsets(sizes, group)) for group in groups)

    def on_device(right_side, phase_mask):
        depth, rows, lanes = right_side.shape
        block = jax.ShapeDtypeStruct((depth, rows, lanes), F32)
        face = (rows, lanes)
        return pl.pallas_call(
            functools.partial(kernel, sizes, groups),
            out_shape=(block, block),
            in_specs=[pl.BlockSpec(memory_space=pltpu.VMEM)] * 2,
            out_specs=(pl.BlockSpec(memory_space=pltpu.VMEM),) * 2,
            scratch_shapes=[
                pltpu.VMEM((ITERS + 1, depth, *face), F32),
                pltpu.VMEM((depth, *face), F32),
                pltpu.VMEM((6, depth, *face), F32),
                pltpu.VMEM((depth, *face), F32),
                pltpu.VMEM((2, 2, *face), jnp.bfloat16),
                pltpu.VMEM((2, 2, depth, lanes), F32),
                pltpu.VMEM((2, 2, *face), jnp.bfloat16),
                pltpu.VMEM((2, 2, depth, lanes), F32),
                pltpu.VMEM((ITERS - 1, 2, depth, lanes), F32),
                pltpu.VMEM((ITERS, *face), F32),
                pltpu.VMEM((ITERS - 1, 2, *face), F32),
                pltpu.VMEM((ITERS - 1, 2, depth, lanes), F32),
                pltpu.VMEM((ITERS, 2, *face), F32),
                pltpu.VMEM((len(groups), 8, lanes), F32),
                pltpu.VMEM((slots, 8, lanes), F32),
                pltpu.SemaphoreType.DMA((ITERS, 6)),
                pltpu.SemaphoreType.DMA((ITERS, 6)),
                pltpu.SemaphoreType.DMA((slots,)),
                pltpu.SemaphoreType.DMA((slots,)),
            ],
            compiler_params=pltpu.CompilerParams(collective_id=0, has_side_effects=True),
        )(right_side, phase_mask)

    return jax.shard_map(
        on_device,
        mesh=mesh,
        in_specs=(P("gz", "gx", "gy"), P("gz", "gx", "gy")),
        out_specs=(P("gz", "gx", "gy"), P("gz", "gx", "gy")),
        check_vma=False,
    )
```

time: 219 us -> 31 us (0.14)
  blocking collectives: 122 us -> 0 us
  waiting for transfers between devices: 38.5 us -> 0 us
  starting transfers between devices: 32.4 us -> 0 us
  Pallas kernels: 0 us -> 27.8 us
  other arithmetic: 11.3 us -> 0 us
  between operations: 10.7 us -> 0.65 us
    psum x3 -> x0, blocking collectives: 122 us -> none  [products(): lax.psum((jnp.sum(first * second), jnp.sum(third * fourth)), ('gx', 'gy',...]
    ppermute x24 -> x0, waiting for transfers between devices: 38.5 us -> none  [the longest x12 30.6 us: padded_2(): lax.ppermute(tail, axis, [(i, (i + 1) % count) for i in range(count)])]
    ppermute x24 -> x0, starting transfers between devices: 32.4 us -> none  [the longest x12 19 us: padded_2(): lax.ppermute(head, axis, [((i + 1) % count, i) for i in range(count)])]
    pallas_call x0 -> x1, Pallas kernels: none -> 27.8 us  [on_device(): pl.pallas_call(functools.partial(kernel, sizes, groups), out_shape=(block...]
    reduce_sum x3 -> x0, other arithmetic: 5.16 us -> none  [products(): jnp.sum(third * fourth)]
    div x3 -> x0, other arithmetic: 3.48 us -> none  [the longest x1 1.97 us: on_device(): return (pressure, residual / diagonal)]
  transfers between devices with their start and end apart: 24 -> 0, of which waited for: 17 -> 0; matrix products, arithmetic and copies ran while one was open for 0% -> 0% of each run, Pallas kernels for 0% -> 0%
where the time goes in v1:
time: 31 us; the launch traced here: 30.9 us
  Pallas kernels  27.8 us (90%)
  local copies, waits for them, and re-layouts  2.42 us (8%)
  between operations  0.65 us (2%)
    pallas_call x1, Pallas kernels, on_device(): pl.pallas_call(functools.partial(kernel, sizes, groups), out_shape=(block...  27.8 us
    unnamed x4, local copies, waits for them, and re-layouts  2.42 us

profile of v1, /device:TPU:0, one launch (start us, length us, event | category | flops | bytes accessed | tf_op | source)
XLA Modules:
  0.0 30.9 jit_solution(2609323935546037192)
XLA Ops:
  0.6 27.8 %shard_map.41 = (f32[8,64,128]{2,1,0:T(8,128)}, f32[8,64,128]{2,1,0:T(8,128)}) custom-call(bf16[8,64,128]{2,1,0:T(8,128)(2,1)} %right_ref.1, s32[8,64,128]{2,1,0:T(8,128)} %mask_ref.1), custom_call_target="tpu_custom_call" | custom-call | tf_op jit(solution)/shard_map/pallas_call | solution.py:297
  28.5 0.0 copy-start
  28.5 1.7 %copy.6 = f32[8,64,128]{2,1,0:T(8,128)} copy(f32[8,64,128]{2,1,0:T(8,128)} %get-tuple-element.4) | data formatting | bytes 524288
  30.2 0.0 copy-done
  30.2 0.7 %copy.7 = f32[8,64,128]{2,1,0:T(8,128)} copy(f32[8,64,128]{2,1,0:T(8,128)S(1)} %copy-done) | data formatting | bytes 524288
Async XLA Ops:
  28.5 1.7 %copy-start = (f32[8,64,128]{2,1,0:T(8,128)S(1)}, f32[8,64,128]{2,1,0:T(8,128)}, u32[]{:S(2)}) copy-start(f32[8,64,128]{2,1,0:T(8,128)} %get-tuple-element.5) | copy-start | bytes 786436

commit v2 on v1

--- a/solution.py
+++ b/solution.py
@@ -31,25 +31,20 @@
     return [dict(zip(group, point)) for point in itertools.product(*spans) if any(point)]
 
 
-def exchange(sizes, phase, faces, landings, send_sems, recv_sems):
+def exchange(sizes, phase, axis, faces, landings, send_sems, recv_sems):
+    place = AXES.index(axis)
     copies = []
-    for place, (axis, (low, high), (from_below, from_above)) in enumerate(
-        zip(("gz", "gx", "gy"), faces, landings)
-    ):
-        for side, source, target, offset in (
-            (0, high, from_below, 1),
-            (1, low, from_above, sizes[axis] - 1),
-        ):
-            copy = pltpu.make_async_remote_copy(
-                src_ref=source,
-                dst_ref=target,
-                send_sem=send_sems.at[phase, 2 * place + side],
-                recv_sem=recv_sems.at[phase, 2 * place + side],
-                device_id=shifted(sizes, {axis: offset}),
-                device_id_type=MESH,
-            )
-            copy.start()
-            copies.append(copy)
+    for side, offset in ((0, 1), (1, sizes[axis] - 1)):
+        copy = pltpu.make_async_remote_copy(
+            src_ref=faces[1 - side],
+            dst_ref=landings[side],
+            send_sem=send_sems.at[phase, 2 * place + side],
+            recv_sem=recv_sems.at[phase, 2 * place + side],
+            device_id=shifted(sizes, {axis: offset}),
+            device_id_type=MESH,
+        )
+        copy.start()
+        copies.append(copy)
     return copies
 
 
@@ -93,9 +88,9 @@
 
 
 def kernel(
-    sizes, groups, right_ref, mask_ref, pressure_ref, scaled_ref,
-    fields, phases, coefs, diag, sz0, sx0, rz0, rx0, sx, sy, rz, rx, ry,
-    partial, gathered, send_sems, recv_sems, sum_send, sum_recv,
+    sizes, groups, right_hbm, mask_hbm, pressure_ref, scaled_ref,
+    right_ref, mask_ref, fields, phases, coefs, diag, sz0, sx0, rz0, rx0, sx, sy, rz, rx, ry,
+    partial, gathered, load_sems, send_sems, recv_sems, sum_send, sum_recv,
 ):
     depth, rows, lanes = right_ref.shape
     peers = []
@@ -107,6 +102,12 @@
     barrier = pltpu.get_barrier_semaphore()
     for offset in peers:
         pl.semaphore_signal(barrier, inc=1, device_id=shifted(sizes, offset), device_id_type=MESH)
+    loads = [
+        pltpu.make_async_copy(mask_hbm, mask_ref, load_sems.at[0]),
+        pltpu.make_async_copy(right_hbm, right_ref, load_sems.at[1]),
+    ]
+    for load in loads:
+        load.start()
 
     row = lax.broadcasted_iota(jnp.int32, (rows, lanes), 0)
     lane = lax.broadcasted_iota(jnp.int32, (rows, lanes), 1)
@@ -132,6 +133,15 @@
             jnp.where(lane == lanes - 1, edge, pltpu.roll(plane, lanes - 1, 1)),
         )
 
+    for load in loads:
+        load.wait()
+    for side, z in ((0, 0), (1, depth - 1)):
+        sz0[side, 0] = right_ref[z]
+        sz0[side, 1] = mask_ref[z].astype(F32).astype(jnp.bfloat16)
+    pl.semaphore_wait(barrier, len(peers))
+    z_copies = exchange(
+        sizes, 0, "gz", (sz0.at[0], sz0.at[1]), (rz0.at[0], rz0.at[1]), send_sems, recv_sems
+    )
     packed = jnp.zeros((rows, lanes), F32)
     for z in range(depth):
         value = right_ref[z].astype(F32)
@@ -143,33 +153,29 @@
         for part, plane in enumerate((value, phase)):
             sx0[0, part, z : z + 1, :] = plane[0:1]
             sx0[1, part, z : z + 1, :] = plane[rows - 1 : rows]
-        for side, face in ((0, 0), (1, depth - 1)):
-            if z == face:
-                sz0[side, 0] = right_ref[z]
-                sz0[side, 1] = phase.astype(jnp.bfloat16)
     sy[0] = packed
-    pl.semaphore_wait(barrier, len(peers))
-
-    copies = exchange(
-        sizes,
-        0,
-        ((sz0.at[0], sz0.at[1]), (sx0.at[0], sx0.at[1]), (sy.at[0], sy.at[0])),
-        ((rz0.at[0], rz0.at[1]), (rx0.at[0], rx0.at[1]), (ry.at[0, 0], ry.at[0, 1])),
-        send_sems,
-        recv_sems,
+    y_copies = exchange(
+        sizes, 0, "gy", (sy.at[0], sy.at[0]), (ry.at[0, 0], ry.at[0, 1]), send_sems, recv_sems
     )
-    for copy in copies:
-        copy.wait()
+    x_copies = exchange(
+        sizes, 0, "gx", (sx0.at[0], sx0.at[1]), (rx0.at[0], rx0.at[1]), send_sems, recv_sems
+    )
 
     def fold(product):
         return jnp.sum(product.reshape(rows // 8, 8, lanes), axis=0)
 
     sums = [jnp.zeros((8, lanes), F32) for _ in range(2 * ITERS)]
     mixed = 2.0 / (density_gas + density_liquid)
+    inner = list(range(1, depth - 1))
     for phase in range(ITERS):
+        for copy in y_copies + x_copies:
+            copy.wait()
         sides = unpack(ry[phase, 0], ry[phase, 1])
         packed = jnp.zeros((rows, lanes), F32)
-        for z in range(depth):
+        for z in inner + [0, depth - 1]:
+            if z == 0:
+                for copy in z_copies:
+                    copy.wait()
             if phase == 0:
                 below = rz0[0, 1].astype(F32) if z == 0 else phases[z - 1]
                 above = rz0[1, 1].astype(F32) if z == depth - 1 else phases[z + 1]
@@ -217,30 +223,31 @@
                 sx[phase, 0, z : z + 1, :] = mean[0:1]
                 sx[phase, 1, z : z + 1, :] = mean[rows - 1 : rows]
         if phase + 1 < ITERS:
+            z_copies = exchange(
+                sizes, phase + 1, "gz",
+                (fields.at[phase + 1, 0], fields.at[phase + 1, depth - 1]),
+                (rz.at[phase, 0], rz.at[phase, 1]),
+                send_sems, recv_sems,
+            )
             sy[phase + 1] = packed
-            copies = exchange(
-                sizes,
-                phase + 1,
-                (
-                    (fields.at[phase + 1, 0], fields.at[phase + 1, depth - 1]),
-                    (sx.at[phase, 0], sx.at[phase, 1]),
-                    (sy.at[phase + 1], sy.at[phase + 1]),
-                ),
-                (
-                    (rz.at[phase, 0], rz.at[phase, 1]),
-                    (rx.at[phase, 0], rx.at[phase, 1]),
-                    (ry.at[phase + 1, 0], ry.at[phase + 1, 1]),
-                ),
-                send_sems,
-                recv_sems,
+            y_copies = exchange(
+                sizes, phase + 1, "gy",
+                (sy.at[phase + 1], sy.at[phase + 1]),
+                (ry.at[phase + 1, 0], ry.at[phase + 1, 1]),
+                send_sems, recv_sems,
             )
-            for copy in copies:
-                copy.wait()
-
-    line = lax.broadcasted_iota(jnp.int32, (8, lanes), 0)
-    tile = jnp.zeros((8, lanes), F32)
+            x_copies = exchange(
+                sizes, phase + 1, "gx",
+                (sx.at[phase, 0], sx.at[phase, 1]),
+                (rx.at[phase, 0], rx.at[phase, 1]),
+                send_sems, recv_sems,
+            )
+
+    place = lax.broadcasted_iota(jnp.int32, (1, lanes), 1)
+    tile = jnp.zeros((1, lanes), F32)
     for k, total in enumerate(sums):
-        tile = jnp.where(line == k, jnp.sum(total, axis=0, keepdims=True), tile)
+        line = jnp.sum(total, axis=0, keepdims=True)
+        tile = jnp.where(place == k, jnp.sum(line, axis=1, keepdims=True), tile)
     slot = 0
     for number, group in enumerate(groups):
         partial[number] = tile
@@ -263,8 +270,7 @@
         for k in range(first, slot):
             tile = tile + gathered[k]
 
-    whole = jnp.sum(tile, axis=1, keepdims=True)
-    moments = [whole[k : k + 1] for k in range(2 * ITERS)]
+    moments = [tile[:, k : k + 1] for k in range(2 * ITERS)]
     pressure, residual = gradient_coefficients(moments)
     for z in range(depth):
         basis = [fields[k, z] for k in range(ITERS + 1)]
@@ -287,7 +293,7 @@
 
 def solution(mesh):
     sizes = {axis: mesh.shape[axis] for axis in AXES}
-    groups = choose_groups(sizes, 8)
+    groups = choose_groups(sizes, 32)
     slots = sum(len(group_offsets(sizes, group)) for group in groups)
 
     def on_device(right_side, phase_mask):
@@ -297,9 +303,11 @@
         return pl.pallas_call(
             functools.partial(kernel, sizes, groups),
             out_shape=(block, block),
-            in_specs=[pl.BlockSpec(memory_space=pltpu.VMEM)] * 2,
+            in_specs=[pl.BlockSpec(memory_space=pltpu.HBM)] * 2,
             out_specs=(pl.BlockSpec(memory_space=pltpu.VMEM),) * 2,
             scratch_shapes=[
+                pltpu.VMEM((depth, *face), jnp.bfloat16),
+                pltpu.VMEM((depth, *face), jnp.int32),
                 pltpu.VMEM((ITERS + 1, depth, *face), F32),
                 pltpu.VMEM((depth, *face), F32),
                 pltpu.VMEM((6, depth, *face), F32),
@@ -313,14 +321,15 @@
                 pltpu.VMEM((ITERS - 1, 2, *face), F32),
                 pltpu.VMEM((ITERS - 1, 2, depth, lanes), F32),
                 pltpu.VMEM((ITERS, 2, *face), F32),
-                pltpu.VMEM((len(groups), 8, lanes), F32),
-                pltpu.VMEM((slots, 8, lanes), F32),
+                pltpu.VMEM((len(groups), 1, lanes), F32),
+                pltpu.VMEM((slots, 1, lanes), F32),
+                pltpu.SemaphoreType.DMA((2,)),
                 pltpu.SemaphoreType.DMA((ITERS, 6)),
                 pltpu.SemaphoreType.DMA((ITERS, 6)),
                 pltpu.SemaphoreType.DMA((slots,)),
                 pltpu.SemaphoreType.DMA((slots,)),
             ],
-            compiler_params=pltpu.CompilerParams(collective_id=0, has_side_effects=True),
+            compiler_params=pltpu.CompilerParams(collective_id=0, has_side_effects=True, vmem_limit_bytes=16 * 2**20),
         )(right_side, phase_mask)
 
     return jax.shard_map(

time: 31 us -> 28.9 us (0.932)
  Pallas kernels: 27.8 us -> 24.8 us
  local copies, waits for them, and re-layouts: 2.42 us -> 3.25 us
    pallas_call x1, Pallas kernels: 27.8 us -> 24.8 us  [on_device(): pl.pallas_call(functools.partial(kernel, sizes, groups), out_shape=(block...]
    unnamed x4 -> x6, local copies, waits for them, and re-layouts: 2.42 us -> 3.25 us
where the time goes in v2:
time: 28.9 us; the launch traced here: 28.8 us
  Pallas kernels  24.8 us (86%)
  local copies, waits for them, and re-layouts  3.25 us (11%)
  between operations  0.65 us (2%)
    pallas_call x1, Pallas kernels, on_device(): pl.pallas_call(functools.partial(kernel, sizes, groups), out_shape=(block...  24.8 us
    unnamed x6, local copies, waits for them, and re-layouts  3.25 us

profile of v2, /device:TPU:0, one launch (start us, length us, event | category | flops | bytes accessed | tf_op | source)
XLA Modules:
  0.0 28.8 jit_solution(9249956365474243577)
XLA Ops:
  0.6 0.0 copy-start
  0.6 0.9 %copy-done = s32[8,64,128]{2,1,0:T(8,128)S(1)} copy-done((s32[8,64,128]{2,1,0:T(8,128)S(1)}, s32[8,64,128]{2,1,0:T(8,128)}, u32[]{:S(2)}) %copy-start) | copy-done | bytes 262168
  1.6 0.0 copy-start.1
  1.6 0.9 %copy-done.1 = bf16[8,64,128]{2,1,0:T(8,128)(2,1)S(1)} copy-done((bf16[8,64,128]{2,1,0:T(8,128)(2,1)S(1)}, bf16[8,64,128]{2,1,0:T(8,128)(2,1)}, u32[]{:S(2)}) %copy-start.1) | copy-done | bytes 131096
  2.5 24.8 %shard_map.41 = (f32[8,64,128]{2,1,0:T(8,128)S(1)}, f32[8,64,128]{2,1,0:T(8,128)S(1)}) custom-call(bf16[8,64,128]{2,1,0:T(8,128)(2,1)S(1)} %copy-done.1, s32[8,64,128]{2,1,0:T(8,128)S(1)} %copy-done), custom_call_target="tpu_custom_call" | custom-call | tf_op jit(solution)/shard_map/pallas_call | solution.py:303
  27.3 0.7 %copy.6 = f32[8,64,128]{2,1,0:T(8,128)} copy(f32[8,64,128]{2,1,0:T(8,128)S(1)} %get-tuple-element.4) | data formatting | bytes 524288
  28.0 0.7 %copy.7 = f32[8,64,128]{2,1,0:T(8,128)} copy(f32[8,64,128]{2,1,0:T(8,128)S(1)} %get-tuple-element.5) | data formatting | bytes 524288
Async XLA Ops:
  0.6 1.0 %copy-start = (s32[8,64,128]{2,1,0:T(8,128)S(1)}, s32[8,64,128]{2,1,0:T(8,128)}, u32[]{:S(2)}) copy-start(s32[8,64,128]{2,1,0:T(8,128)} %mask_hbm.1) | copy-start | bytes 786436
  1.6 0.9 %copy-start.1 = (bf16[8,64,128]{2,1,0:T(8,128)(2,1)S(1)}, bf16[8,64,128]{2,1,0:T(8,128)(2,1)}, u32[]{:S(2)}) copy-start(bf16[8,64,128]{2,1,0:T(8,128)(2,1)} %right_hbm.1) | copy-start | bytes 393220

commit v3 on v2

--- a/solution.py
+++ b/solution.py
@@ -329,7 +329,7 @@
                 pltpu.SemaphoreType.DMA((slots,)),
                 pltpu.SemaphoreType.DMA((slots,)),
             ],
-            compiler_params=pltpu.CompilerParams(collective_id=0, has_side_effects=True, vmem_limit_bytes=16 * 2**20),
+            compiler_params=pltpu.CompilerParams(collective_id=0, has_side_effects=True, vmem_limit_bytes=54408 * 2**10),
         )(right_side, phase_mask)
 
     return jax.shard_map(

time: 28.9 us -> 28 us (0.969)
  local copies, waits for them, and re-layouts: 3.25 us -> 2.3 us
    unnamed x6 -> x4, local copies, waits for them, and re-layouts: 3.25 us -> 2.3 us
where the time goes in v3:
time: 28 us; the launch traced here: 27.8 us
  Pallas kernels  24.8 us (89%)
  local copies, waits for them, and re-layouts  2.3 us (8%)
  between operations  0.65 us (2%)
    pallas_call x1, Pallas kernels, on_device(): pl.pallas_call(functools.partial(kernel, sizes, groups), out_shape=(block...  24.8 us
    unnamed x4, local copies, waits for them, and re-layouts  2.3 us

profile of v3, /device:TPU:0, one launch (start us, length us, event | category | flops | bytes accessed | tf_op | source)
XLA Modules:
  0.0 27.8 jit_solution(7231454852169421000)
XLA Ops:
  0.6 0.0 copy-start
  0.6 0.9 %copy-done = bf16[8,64,128]{2,1,0:T(8,128)(2,1)S(1)} copy-done((bf16[8,64,128]{2,1,0:T(8,128)(2,1)S(1)}, bf16[8,64,128]{2,1,0:T(8,128)(2,1)}, u32[]{:S(2)}) %copy-start) | copy-done | bytes 131096
  1.5 24.8 %shard_map.41 = (f32[8,64,128]{2,1,0:T(8,128)S(1)}, f32[8,64,128]{2,1,0:T(8,128)S(1)}) custom-call(bf16[8,64,128]{2,1,0:T(8,128)(2,1)S(1)} %copy-done, s32[8,64,128]{2,1,0:T(8,128)} %mask_hbm.1), custom_call_target="tpu_custom_call" | custom-call | tf_op jit(solution)/shard_map/pallas_call | solution.py:303
  26.4 0.7 %copy.6 = f32[8,64,128]{2,1,0:T(8,128)} copy(f32[8,64,128]{2,1,0:T(8,128)S(1)} %get-tuple-element.4) | data formatting | bytes 524288
  27.1 0.7 %copy.7 = f32[8,64,128]{2,1,0:T(8,128)} copy(f32[8,64,128]{2,1,0:T(8,128)S(1)} %get-tuple-element.5) | data formatting | bytes 524288
Async XLA Ops:
  0.6 0.9 %copy-start = (bf16[8,64,128]{2,1,0:T(8,128)(2,1)S(1)}, bf16[8,64,128]{2,1,0:T(8,128)(2,1)}, u32[]{:S(2)}) copy-start(bf16[8,64,128]{2,1,0:T(8,128)(2,1)} %right_hbm.1) | copy-start | bytes 393220
